TPU v7x, 128 devices: a whole 4x4x4 slice. The times are simulated.
128 devices in a mesh: rows: 32 (over z, x, core), grp: 4 (over y).
Axes of the slice: x: 4, y: 4, z: 4, core: 2. Of those that a mesh axis runs over, the one named last changes fastest.
Arguments:
- tiles: bfloat16 [16384, 128, 128], P(('rows', 'grp')), may hold values from -0.3125 to 0.3125
- tile_rows: int32 [16384], P(('rows', 'grp')), may hold values from 0 to 47, as said below
- tile_cols: int32 [16384], P(('rows', 'grp')), may hold values from 0 to 2047, as said below
- tile_count: int32 [128], P(('rows', 'grp')), may hold values from 32 to 128, as said below
- block_perm: int32 [2048], replicated, may hold values from 0 to 2047, as said below
- panel: bfloat16 [2048, 128, 256], P(('rows', 'grp')), may hold values from -6 to 6
Outputs:
- sketch: bfloat16 [6144, 128, 256], P(('rows', 'grp'))
- gram: float32 [2048, 128, 256], P(('rows', 'grp'))
Inputs may be any that keep to these rules, and one draw needn't show every extreme that they name: `tile_rows`: each device's live tile rows are non-decreasing; slots past the count hold 47. `tile_cols`: among one device's live tiles, those whose block_perm positions lie with one owner (position // 16) name at most 2 distinct column blocks; every device reaches 2 for some owner. `tile_count`: some device has 128 live tiles. `block_perm`: A permutation of the column blocks.
All inputs are finite; a program needn't handle non-finite values.
Results may differ from a plain program's by a relative error of at most 0.0034.
Values may be sent and summed in bfloat16 or wider, within the bound.
No kernel may reach another device: no remote copies, remote signals or barrier semaphores. Data moves between devices by JAX's collectives and lax.ppermute only.
A program may use at most 128 MiB of HBM per device.

v0:
```python
import functools

import jax
import jax.numpy as jnp
from jax import lax
from jax.experimental import pallas as pl
from jax.experimental.pallas import tpu as pltpu
from jax.sharding import PartitionSpec as P

RB_DEV = 48
AXES = ("rows", "grp")
LANES = 128
CHUNK = 8
GROUP_BITS = 3


def distinct_blocks(stored_at, is_live, total_blocks):
    slots = stored_at.shape[0]
    ids = jnp.arange(slots, dtype=jnp.int32)
    same = (stored_at[:, None] == stored_at[None, :]) & is_live[None, :] & is_live[:, None]
    leader = jnp.min(jnp.where(same, ids[None, :], slots), axis=1)
    is_first = leader == ids
    slot_of = jnp.sum((is_first[None, :] & (ids[None, :] < leader[:, None])).astype(jnp.int32), axis=1)
    slot_of = jnp.where(is_live, slot_of, 0)
    at_slot = is_first[None, :] & (slot_of[None, :] == ids[:, None])
    wanted = jnp.max(jnp.where(at_slot, stored_at[None, :], -1), axis=1)
    wanted = jnp.where(wanted < 0, total_blocks, wanted)
    return wanted, slot_of, is_first.astype(jnp.int32)


def gather_kernel(capacity, want_ref, rows_ref, out_ref, table, stage):
    devices, held = rows_ref.shape[0], 16
    blocks = devices * held

    @pl.when(pl.program_id(0) == 0)
    def _():
        for half in range(2):
            rows = rows_ref[:, half * held : (half + 1) * held, :].astype(jnp.float32)
            table[pl.ds(half, blocks, stride=2), :] = rows.reshape(blocks, LANES)

    for local in range(CHUNK):
        for k in range(capacity):
            src = want_ref[0, 0, local * LANES + k]
            stage[pl.ds(2 * (local * capacity + k), 2), :] = table[pl.ds(src, 2), :]
    span = CHUNK * capacity
    out_ref[:, :LANES] = stage[pl.ds(0, span, stride=2), :].astype(jnp.bfloat16)
    out_ref[:, LANES:] = stage[pl.ds(1, span, stride=2), :].astype(jnp.bfloat16)


def want_blocks(devices):
    return pl.BlockSpec((1, 1, CHUNK * LANES), lambda s: (s, 0, 0), memory_space=pltpu.SMEM)


def gather_rows(want, rows, capacity):
    devices = rows.shape[0]
    blocks = devices * 16
    return pl.pallas_call(
        functools.partial(gather_kernel, capacity),
        grid=(devices // CHUNK,),
        in_specs=[want_blocks(devices), pl.BlockSpec(rows.shape, lambda s: (0, 0, 0))],
        out_specs=pl.BlockSpec((CHUNK * capacity, 2 * LANES), lambda s: (s, 0)),
        out_shape=jax.ShapeDtypeStruct((devices * capacity, 2 * LANES), jnp.bfloat16),
        scratch_shapes=[
            pltpu.VMEM((2 * (blocks + 8), LANES), jnp.float32),
            pltpu.VMEM((2 * CHUNK * capacity, LANES), jnp.float32),
        ],
        compiler_params=pltpu.CompilerParams(vmem_limit_bytes=16 << 20),
        name=f"gather_rows_{capacity}",
    )(want, rows)


def product_kernel(
    capacity, slot_ref, first_ref, row_ref, count_ref, tiles_ref, in_ref, sketch_ref, out_ref,
    in_l, in_r, acc
):
    step = pl.program_id(0)
    span = in_ref.shape[0]
    steps_in = LANES * capacity // span

    @pl.when(step < steps_in)
    def _():
        at = pl.multiple_of(step * span, 8)
        in_l[pl.ds(at, span), :] = in_ref[:, :LANES].astype(jnp.float32)
        in_r[pl.ds(at, span), :] = in_ref[:, LANES:].astype(jnp.float32)

    def forward(first_tile, group):
        products = []
        for t in [first_tile + k for k in range(group)]:
            rows = pl.ds(slot_ref[t], LANES, stride=capacity)
            block = jnp.concatenate(
                [in_l[rows, :].astype(jnp.bfloat16), in_r[rows, :].astype(jnp.bfloat16)], axis=1
            )
            products.append(jnp.dot(tiles_ref[t], block, preferred_element_type=jnp.float32))
        total = acc[...]
        for k, product in enumerate(products):
            t = first_tile + k
            row = row_ref[t]
            fresh = (t == 0) | (row_ref[jnp.maximum(t - 1, 0)] != row)
            total = jnp.where(fresh, product, total + product)
            sketch_ref[row] = total.astype(jnp.bfloat16)
        acc[...] = total

    def backward(first_tile, group):
        parts = []
        for t in [first_tile + k for k in range(group)]:
            parts.append(
                lax.dot_general(
                    tiles_ref[t],
                    sketch_ref[row_ref[t]],
                    (((0,), (0,)), ((), ())),
                    preferred_element_type=jnp.float32,
                )
            )
        for k, part in enumerate(parts):
            t = first_tile + k
            rows = pl.ds(slot_ref[t], LANES, stride=capacity)
            first = first_ref[t] == 1
            in_l[rows, :] = part[:, :LANES] + jnp.where(first, 0.0, in_l[rows, :])
            in_r[rows, :] = part[:, LANES:] + jnp.where(first, 0.0, in_r[rows, :])

    @pl.when(step == steps_in)
    def _():
        count = count_ref[0]
        full = lax.shift_right_logical(count, GROUP_BITS)
        group = 1 << GROUP_BITS
        sketch_ref[...] = jnp.zeros_like(sketch_ref)
        for work in (forward, backward):

            def many(g, carry, work=work):
                work(g * group, group)
                return carry

            def single(t, carry, work=work):
                work(t, 1)
                return carry

            lax.fori_loop(0, full, many, 0)
            lax.fori_loop(full * group, count, single, 0)

    @pl.when(step > steps_in)
    def _():
        at = pl.multiple_of((step - steps_in - 1) * span, 8)
        out_ref[:, :LANES] = in_l[pl.ds(at, span), :].astype(jnp.bfloat16)
        out_ref[:, LANES:] = in_r[pl.ds(at, span), :].astype(jnp.bfloat16)


def tile_products(slot_of, is_first, tile_rows, tile_count, tiles, fetched, capacity):
    steps = 8
    span = LANES // steps * capacity
    scalars = [pl.BlockSpec(memory_space=pltpu.SMEM)] * 4
    f32_rows = pltpu.VMEM((LANES * capacity, LANES), jnp.float32)
    return pl.pallas_call(
        functools.partial(product_kernel, capacity),
        grid=(2 * steps + 1,),
        in_specs=scalars
        + [
            pl.BlockSpec(tiles.shape, lambda s: (0, 0, 0), pipeline_mode=pl.Buffered(1)),
            pl.BlockSpec((span, 2 * LANES), lambda s: (jnp.minimum(s, steps - 1), 0)),
        ],
        out_specs=[
            pl.BlockSpec((RB_DEV, LANES, 2 * LANES), lambda s: (0, 0, 0), pipeline_mode=pl.Buffered(1)),
            pl.BlockSpec((span, 2 * LANES), lambda s: (jnp.maximum(s - steps - 1, 0), 0)),
        ],
        out_shape=[
            jax.ShapeDtypeStruct((RB_DEV, LANES, 2 * LANES), jnp.bfloat16),
            jax.ShapeDtypeStruct((LANES * capacity, 2 * LANES), jnp.bfloat16),
        ],
        scratch_shapes=[
            f32_rows,
            f32_rows,
            pltpu.VMEM((LANES, 2 * LANES), jnp.float32),
        ],
        compiler_params=pltpu.CompilerParams(vmem_limit_bytes=36 << 20),
        name=f"tile_products_{capacity}",
    )(slot_of, is_first, tile_rows, tile_count, tiles, fetched)


def sum_kernel(capacity, want_ref, in_ref, out_ref, total, stage):
    step = pl.program_id(0)
    span = CHUNK * capacity

    @pl.when(step == 0)
    def _():
        total[...] = jnp.zeros_like(total)

    stage[pl.ds(0, span, stride=2), :] = in_ref[:, :LANES].astype(jnp.float32)
    stage[pl.ds(1, span, stride=2), :] = in_ref[:, LANES:].astype(jnp.float32)
    for local in range(CHUNK):

        def load(g, local=local):
            loaded = []
            for k in range(g * 8, g * 8 + 8):
                w = want_ref[0, 0, local * LANES + k]
                loaded.append((w, total[pl.ds(w, 2), :], stage[pl.ds(2 * (local * capacity + k), 2), :]))
            return loaded

        ahead = load(0)
        for g in range(capacity // 8):
            now, ahead = ahead, load(g + 1) if g + 1 < capacity // 8 else None
            for w, old, row in now:
                total[pl.ds(w, 2), :] = old + row

    @pl.when(step == pl.num_programs(0) - 1)
    def _():
        blocks = out_ref.shape[0]
        out_ref[:, :LANES] = total[pl.ds(0, blocks, stride=2), :].astype(jnp.bfloat16)
        out_ref[:, LANES:] = total[pl.ds(1, blocks, stride=2), :].astype(jnp.bfloat16)


def sum_rows(want, inbound, capacity, devices):
    blocks = devices * 16
    return pl.pallas_call(
        functools.partial(sum_kernel, capacity),
        grid=(devices // CHUNK,),
        in_specs=[want_blocks(devices), pl.BlockSpec((CHUNK * capacity, 2 * LANES), lambda s: (s, 0))],
        out_specs=pl.BlockSpec((blocks, 2 * LANES), lambda s: (0, 0)),
        out_shape=jax.ShapeDtypeStruct((blocks, 2 * LANES), jnp.bfloat16),
        scratch_shapes=[
            pltpu.VMEM((2 * (blocks + 8), LANES), jnp.float32),
            pltpu.VMEM((2 * CHUNK * capacity, LANES), jnp.float32),
        ],
        compiler_params=pltpu.CompilerParams(vmem_limit_bytes=16 << 20),
        name=f"sum_rows_{capacity}",
    )(want, inbound)


def exchange(x):
    return lax.all_to_all(x, AXES, split_axis=0, concat_axis=0, tiled=True)


def per_device(tiles, tile_rows, tile_cols, tile_count, block_perm, panel):
    devices = lax.axis_size(AXES)
    held = panel.shape[0]
    blocks = devices * held
    slot_ids = jnp.arange(tiles.shape[0], dtype=jnp.int32)
    is_live = slot_ids < tile_count[0]
    stored_at = block_perm[tile_cols]
    wanted, slot_of, is_first = distinct_blocks(stored_at, is_live, blocks)

    digits = jnp.stack([wanted // held, wanted % held]).astype(jnp.bfloat16)
    stripes = panel.reshape(held, devices, 2, LANES).transpose(1, 2, 0, 3).reshape(devices, 2 * held, LANES)
    stripes = jnp.concatenate([stripes, jnp.broadcast_to(digits[None], (devices, 2, LANES))], axis=1)
    striped = exchange(stripes)
    lists = striped[:, 2 * held :, :].astype(jnp.int32)
    want = (lists[:, 0] * held + lists[:, 1])
    counts = jnp.sum((want < blocks).astype(jnp.int32), axis=1)
    want = (2 * want).reshape(devices // CHUNK, 1, CHUNK * LANES)

    def with_capacity(capacity):
        def run():
            outgoing = gather_rows(want, striped, capacity)
            fetched = exchange(outgoing.reshape(devices, capacity, 2 * LANES))
            sketch, outbound = tile_products(
                slot_of, is_first, tile_rows, tile_count, tiles,
                fetched.reshape(devices * capacity, 2 * LANES), capacity,
            )
            inbound = exchange(outbound.reshape(devices, capacity, 2 * LANES))
            summed = sum_rows(want, inbound.reshape(devices * capacity, 2 * LANES), capacity, devices)
            return sketch, summed

        return run

    sketch, summed = lax.cond(jnp.max(counts) <= 112, with_capacity(112), with_capacity(128))
    gram = exchange(summed.reshape(devices, held, 2 * LANES))
    return sketch, gram.transpose(1, 0, 2).astype(jnp.float32)


def solution(mesh):
    split = P(AXES, None, None)
    line = P(AXES)
    return jax.shard_map(
        per_device,
        mesh=mesh,
        in_specs=(split, line, line, line, P(), split),
        out_specs=(split, split),
        check_vma=False,
    )
```

profile of v0, /device:TPU:1, one launch (start us, length us, event | category | flops | bytes accessed | tf_op | source)
XLA Modules:
  0.0 322.2 jit_solution(11158562817212662080)
XLA Ops:
  0.6 0.0 copy-start
  1.3 0.7 compare_select_fusion.1
  2.0 0.0 copy-done
  2.0 1.1 gather_fusion
  3.1 0.2 select_reduce_fusion.1
  3.3 0.2 convert_reduce_fusion
  3.5 0.1 select_reduce_fusion
  3.7 1.3 reshape.187
  5.0 1.2 copy.11
  6.3 0.0 copy-start.4
  6.3 0.2 pad_maximum_fusion
  6.5 33.4 %all_to_all.30 = bf16[128,34,128]{2,1,0:T(8,128)(2,1)S(1)} all-to-all(bf16[128,34,128]{2,1,0:T(8,128)(2,1)S(1)} %pad_maximum_fusion), channel_id=1, replica_groups=mesh['rows'=32,'grp'=4] {'rows','grp'}, dimensions={0} | all-to-all | bytes 2228224 | tf_op jit(solution)/shard_map/all_to_all | solution.py:228
  39.9 0.1 slice_convert_fusion
  39.9 0.1 broadcast_multiply_fusion
  40.1 2.4 fusion
  42.4 0.6 reduce_max.22
  43.7 0.0 copy-done.4
  43.7 252.5 %conditional.1 = (bf16[48,128,256]{2,1,0:T(8,128)(2,1)}, bf16[2048,256]{1,0:T(8,128)(2,1)S(1)}) conditional(s32[]{:T(128)} %convert_element_type.30, (s32[16,1,1024]{2,1,0:T(1,128)S(1)}, bf16[128,34,128]{2,1,0:T(8,128)(2,1)S(1)}, s32[128]{0:T(128)S(1)}, s32[128]{0:T(128)S(1)}, s32[128]{0:T(128)S(1)}, /*index=5*/s32[1]{0:T(128)}, ...), branch_computations={%region_5.6_spmd, %region_6.7_spmd} | conditional | bytes 50331692 | solution.py:263
  43.9 13.5 %gather_rows_112.1 = bf16[14336,256]{1,0:T(8,128)(2,1)S(1)} custom-call(s32[16,1,1024]{2,1,0:T(1,128)S(1)} %get-tuple-element.42.want_ref, bf16[128,34,128]{2,1,0:T(8,128)(2,1)S(1)} %get-tuple-element.43.rows_ref), custom_call_target="tpu_custom_call" | custom-call | tf_op jit(solution)/shard_map/cond/branch_1_fun/gather_rows_112/pallas_call | solution.py:57
  57.4 0.0 copy-start.3
  57.4 90.4 %all_to_all.28 = bf16[128,112,256]{2,1,0:T(8,128)(2,1)S(1)} all-to-all(bf16[128,112,256]{2,1,0:T(8,128)(2,1)S(1)} %bitcast.33), channel_id=1, replica_groups=mesh['rows'=32,'grp'=4] {'rows','grp'}, dimensions={0} | all-to-all | bytes 14680064 | tf_op jit(solution)/shard_map/cond/branch_1_fun/all_to_all | solution.py:228
  147.8 0.0 copy-done.3
  147.8 31.7 %tile_products_112.1 = (bf16[48,128,256]{2,1,0:T(8,128)(2,1)}, bf16[14336,256]{1,0:T(8,128)(2,1)S(1)}) custom-call(s32[128]{0:T(128)S(1)} %get-tuple-element.37.slot_ref, s32[128]{0:T(128)S(1)} %get-tuple-element.38.first_ref, s32[128]{0:T(128)S(1)} %get-tuple-element.39.row_ref, s32[1]{0:T(128)} %get-tuple-element.40.count_ref, ...), custom_call_target="tpu_custom_call" | custom-call | tf_op jit(solution)/shard_map/cond/branch_1_fun/tile_products_112/pallas_call | solution.py:152
  179.5 94.5 %all_to_all.29 = bf16[128,112,256]{2,1,0:T(8,128)(2,1)S(1)} all-to-all(bf16[128,112,256]{2,1,0:T(8,128)(2,1)S(1)} %bitcast.35), channel_id=1, replica_groups=mesh['rows'=32,'grp'=4] {'rows','grp'}, dimensions={0} | all-to-all | bytes 14680064 | tf_op jit(solution)/shard_map/cond/branch_1_fun/all_to_all | solution.py:228
  274.0 22.3 %sum_rows_112.1 = bf16[2048,256]{1,0:T(8,128)(2,1)S(1)} custom-call(s32[16,1,1024]{2,1,0:T(1,128)S(1)} %get-tuple-element.42.want_ref, bf16[14336,256]{1,0:T(8,128)(2,1)S(1)} %bitcast.32), custom_call_target="tpu_custom_call" | custom-call | tf_op jit(solution)/shard_map/cond/branch_1_fun/sum_rows_112/pallas_call | solution.py:212
  296.2 0.0 copy-start.1
  296.3 23.1 %all_to_all.31 = bf16[128,16,256]{2,1,0:T(8,128)(2,1)S(1)} all-to-all(bf16[128,16,256]{2,1,0:T(8,128)(2,1)S(1)} %bitcast.36), channel_id=1, replica_groups=mesh['rows'=32,'grp'=4] {'rows','grp'}, dimensions={0} | all-to-all | bytes 2097152 | tf_op jit(solution)/shard_map/all_to_all | solution.py:228
  319.4 0.3 convert_bitcast_fusion
  319.7 2.5 copy.12
  322.2 0.0 copy-done.1
  (7 shorter events, 0.1 us)
Async XLA Ops:
  0.6 1.4 copy-start
  6.3 37.5 %copy-start.4 = (s32[128]{0:T(128)S(1)}, s32[128]{0:T(128)}, u32[]{:S(2)}) copy-start(s32[128]{0:T(128)} %param.9) | copy-start | bytes 1540
  57.4 90.4 %copy-start.3 = (bf16[128,128,128]{2,1,0:T(8,128)(2,1)S(1)}, bf16[128,128,128]{2,1,0:T(8,128)(2,1)}, u32[]{:S(2)}) copy-start(bf16[128,128,128]{2,1,0:T(8,128)(2,1)} %get-tuple-element.41.tiles_ref) | copy-start | bytes 12582916 | tf_op jit(solution)/shard_map/cond
  296.2 26.0 %copy-start.1 = (s32[2048]{0:T(1024)S(1)}, s32[2048]{0:T(1024)}, u32[]{:S(2)}) copy-start(s32[2048]{0:T(1024)} %param.12) | copy-start | bytes 24580
where the time goes:
time: 322 us
  blocking collectives  241 us (75%)
  Pallas kernels  67.5 us (21%)
  local copies, waits for them, and re-layouts  6.32 us (2%)
  other arithmetic  4.8 us (1%)
    all_to_all x4, blocking collectives, exchange(): return lax.all_to_all(x, AXES, split_axis=0, concat_axis=0, tiled=True)  241 us
    pallas_call x1, Pallas kernels, tile_products(): pl.pallas_call(functools.partial(product_kernel, capacity), grid=(2 * ste...  31.7 us
    pallas_call x1, Pallas kernels, sum_rows(): pl.pallas_call(functools.partial(sum_kernel, capacity), grid=(devices //...  22.3 us
    pallas_call x1, Pallas kernels, gather_rows(): pl.pallas_call(functools.partial(gather_kernel, capacity), grid=(devices...  13.5 us

commit v1 on v0

v1 whole, which is shorter than its diff:
```python
import functools

import jax
import jax.numpy as jnp
from jax import lax
from jax.experimental import pallas as pl
from jax.experimental.pallas import tpu as pltpu
from jax.sharding import PartitionSpec as P

RB_DEV = 48
AXES = ("rows", "grp")
LANES = 128
CHUNK = 8
GROUP_BITS = 3
SUM_GROUP = 8
GRANT = 12
PRODUCT_GRANT = 24
CAPACITIES = (104, 112, 128)


def distinct_blocks(stored_at, is_live, total_blocks):
    slots = stored_at.shape[0]
    ids = jnp.arange(slots, dtype=jnp.int32)
    same = (stored_at[:, None] == stored_at[None, :]) & is_live[None, :] & is_live[:, None]
    leader = jnp.min(jnp.where(same, ids[None, :], slots), axis=1)
    is_first = leader == ids
    slot_of = jnp.sum((is_first[None, :] & (ids[None, :] < leader[:, None])).astype(jnp.int32), axis=1)
    slot_of = jnp.where(is_live, slot_of, 0)
    at_slot = is_first[None, :] & (slot_of[None, :] == ids[:, None])
    wanted = jnp.max(jnp.where(at_slot, stored_at[None, :], -1), axis=1)
    wanted = jnp.where(wanted < 0, total_blocks, wanted)
    return wanted, slot_of, is_first.astype(jnp.int32)


def chunk_lists(want_ref, buffers, semaphores, work):
    chunks = want_ref.shape[0]

    def copy(chunk, side):
        return pltpu.make_async_copy(want_ref.at[chunk], buffers[side], semaphores.at[side])

    for side in range(2):
        copy(side, side).start()

    def pair(p, carry):
        for side in range(2):
            chunk = 2 * p + side
            copy(chunk, side).wait()
            work(chunk, buffers[side])

            @pl.when(chunk + 2 < chunks)
            def _(chunk=chunk, side=side):
                copy(chunk + 2, side).start()

        return carry

    lax.fori_loop(0, chunks // 2, pair, 0)


def spans(capacity):
    marks = [0] + [m for m in (56, 80) if m < capacity] + [capacity]
    return list(zip(marks[:-1], marks[1:]))


def when_listed(listed, local, start, absent, work):
    if start == 0:
        work()
    else:
        pl.when(listed[local, start] < absent)(work)


def gather_kernel(capacity, want_ref, rows_ref, out_ref, table, stage, list_a, list_b, semaphores):
    devices, held = rows_ref.shape[0], 16
    blocks = devices * held
    span = CHUNK * capacity
    for half in range(2):
        rows = rows_ref[:, half * held : (half + 1) * held, :].astype(jnp.float32)
        table[pl.ds(half, blocks, stride=2), :] = rows.reshape(blocks, LANES)

    def work(chunk, listed):
        for local in range(CHUNK):
            for start, stop in spans(capacity):

                def rows(local=local, start=start, stop=stop):
                    for k in range(start, stop):
                        src = listed[local, k]
                        stage[pl.ds(2 * (local * capacity + k), 2), :] = table[pl.ds(src, 2), :]

                when_listed(listed, local, start, 2 * blocks, rows)
        at = pl.multiple_of(chunk * span, 16)
        out_ref[pl.ds(at, span), :LANES] = stage[pl.ds(0, span, stride=2), :].astype(jnp.bfloat16)
        out_ref[pl.ds(at, span), LANES:] = stage[pl.ds(1, span, stride=2), :].astype(jnp.bfloat16)

    chunk_lists(want_ref, (list_a, list_b), semaphores, work)


def row_scratch(blocks, capacity, tables=1):
    lists = pltpu.SMEM((CHUNK, LANES), jnp.int32)
    table = pltpu.VMEM((2 * (blocks + 8), LANES), jnp.float32)
    return [table] * tables + [
        pltpu.VMEM((2 * CHUNK * capacity, LANES), jnp.float32),
        lists,
        lists,
        pltpu.SemaphoreType.DMA((2,)),
    ]


def gather_rows(want, rows, capacity):
    devices = rows.shape[0]
    return pl.pallas_call(
        functools.partial(gather_kernel, capacity),
        in_specs=[pl.BlockSpec(memory_space=pl.ANY), pl.BlockSpec(memory_space=pltpu.VMEM)],
        out_specs=pl.BlockSpec(memory_space=pltpu.VMEM),
        out_shape=jax.ShapeDtypeStruct((devices * capacity, 2 * LANES), jnp.bfloat16),
        scratch_shapes=row_scratch(devices * 16, capacity),
        compiler_params=pltpu.CompilerParams(vmem_limit_bytes=GRANT << 20),
        name=f"gather_rows_{capacity}",
    )(want, rows)


def product_kernel(
    capacity, slot_ref, first_ref, row_ref, count_ref, tiles_ref, in_ref, sketch_ref, out_ref,
    in_l, in_r, acc, sketch, sent
):
    stride = capacity + 1
    count = count_ref[0]
    full = lax.shift_right_logical(count, GROUP_BITS)
    group = 1 << GROUP_BITS
    halves = ((in_l, pl.ds(0, LANES)), (in_r, pl.ds(LANES, LANES)))

    def spread(c, carry):
        for k in range(CHUNK):
            source = pl.ds(pl.multiple_of((c * CHUNK + k) * capacity, 8), capacity)
            for half, lanes in halves:
                half[pl.ds((c * CHUNK + k) * stride, capacity), :] = in_ref[source, lanes].astype(jnp.float32)
        return carry

    def pack(c, carry):
        for k in range(CHUNK):
            target = pl.ds(pl.multiple_of((c * CHUNK + k) * capacity, 8), capacity)
            for half, lanes in halves:
                out_ref[target, lanes] = half[pl.ds((c * CHUNK + k) * stride, capacity), :].astype(jnp.bfloat16)
        return carry

    def forward(first_tile, group):
        products = []
        for t in [first_tile + k for k in range(group)]:
            rows = pl.ds(slot_ref[t], LANES, stride=stride)
            block = jnp.concatenate([half[rows, :].astype(jnp.bfloat16) for half, _ in halves], axis=1)
            products.append(jnp.dot(tiles_ref[t], block, preferred_element_type=jnp.float32))
        total = acc[...]
        for k, product in enumerate(products):
            t = first_tile + k
            row = row_ref[t]
            fresh = (t == 0) | (row_ref[jnp.maximum(t - 1, 0)] != row)
            total = jnp.where(fresh, product, total + product)
            sketch[row] = total.astype(jnp.bfloat16)
        acc[...] = total

    def backward(first_tile, group):
        parts = []
        for t in [first_tile + k for k in range(group)]:
            parts.append(
                lax.dot_general(
                    tiles_ref[t],
                    sketch[row_ref[t]],
                    (((0,), (0,)), ((), ())),
                    preferred_element_type=jnp.float32,
                )
            )
        for k, part in enumerate(parts):
            t = first_tile + k
            rows = pl.ds(slot_ref[t], LANES, stride=stride)
            first = first_ref[t] == 1
            for (half, _), piece in zip(halves, (part[:, :LANES], part[:, LANES:])):
                half[rows, :] = piece + jnp.where(first, 0.0, half[rows, :])

    def over_tiles(work):
        def many(g, carry):
            work(g * group, group)
            return carry

        def single(t, carry):
            work(t, 1)
            return carry

        lax.fori_loop(0, full, many, 0)
        lax.fori_loop(full * group, count, single, 0)

    sketch[...] = jnp.zeros_like(sketch)
    lax.fori_loop(0, LANES // CHUNK, spread, 0)
    over_tiles(forward)
    send = pltpu.make_async_copy(sketch, sketch_ref, sent)
    send.start()
    over_tiles(backward)
    lax.fori_loop(0, LANES // CHUNK, pack, 0)
    send.wait()


def tile_products(slot_of, is_first, tile_rows, tile_count, tiles, fetched, capacity):
    f32_rows = pltpu.VMEM((LANES * (capacity + 1), LANES), jnp.float32)
    sketch = (RB_DEV, LANES, 2 * LANES)
    return pl.pallas_call(
        functools.partial(product_kernel, capacity),
        in_specs=[pl.BlockSpec(memory_space=pltpu.SMEM)] * 4
        + [pl.BlockSpec(memory_space=pltpu.VMEM)] * 2,
        out_specs=[pl.BlockSpec(memory_space=pl.ANY), pl.BlockSpec(memory_space=pltpu.VMEM)],
        out_shape=[
            jax.ShapeDtypeStruct(sketch, jnp.bfloat16),
            jax.ShapeDtypeStruct((LANES * capacity, 2 * LANES), jnp.bfloat16),
        ],
        scratch_shapes=[
            f32_rows,
            f32_rows,
            pltpu.VMEM((LANES, 2 * LANES), jnp.float32),
            pltpu.VMEM(sketch, jnp.bfloat16),
            pltpu.SemaphoreType.DMA,
        ],
        compiler_params=pltpu.CompilerParams(vmem_limit_bytes=PRODUCT_GRANT << 20),
        name=f"tile_products_{capacity}",
    )(slot_of, is_first, tile_rows, tile_count, tiles, fetched)


def sum_kernel(capacity, want_ref, in_ref, out_ref, even, odd, stage, list_a, list_b, semaphores):
    span = CHUNK * capacity
    blocks = out_ref.shape[0]
    even[...] = jnp.zeros_like(even)
    odd[...] = jnp.zeros_like(odd)

    def work(chunk, listed):
        at = pl.multiple_of(chunk * span, 16)
        stage[pl.ds(0, span, stride=2), :] = in_ref[pl.ds(at, span), :LANES].astype(jnp.float32)
        stage[pl.ds(1, span, stride=2), :] = in_ref[pl.ds(at, span), LANES:].astype(jnp.float32)
        for local in range(0, CHUNK, 2):
            totals = (even, odd)

            def load(side, g, stop, local=local):
                loaded = []
                for k in range(g, min(g + SUM_GROUP, stop)):
                    w = listed[local + side, k]
                    row = stage[pl.ds(2 * ((local + side) * capacity + k), 2), :]
                    loaded.append((w, totals[side][pl.ds(w, 2), :], row))
                return loaded

            def store(side, loaded):
                for w, old, row in loaded:
                    totals[side][pl.ds(w, 2), :] = old + row

            for start, stop in spans(capacity):

                def rows(start=start, stop=stop, load=load):
                    last = load(0, start, stop)
                    turns = [(side, g) for g in range(start, stop, SUM_GROUP) for side in range(2)]
                    for here, ahead in zip(turns, turns[1:] + [None]):
                        following = load(*ahead, stop) if ahead else None
                        store(here[0], last)
                        last = following

                if start == 0:
                    rows()
                else:
                    longest = jnp.minimum(listed[local, start], listed[local + 1, start])
                    pl.when(longest < 2 * blocks)(rows)

    chunk_lists(want_ref, (list_a, list_b), semaphores, work)
    for half in range(2):
        rows = pl.ds(half, blocks, stride=2)
        out_ref[:, half * LANES : (half + 1) * LANES] = (even[rows, :] + odd[rows, :]).astype(jnp.bfloat16)


def sum_rows(want, inbound, capacity, devices):
    blocks = devices * 16
    return pl.pallas_call(
        functools.partial(sum_kernel, capacity),
        in_specs=[pl.BlockSpec(memory_space=pl.ANY), pl.BlockSpec(memory_space=pltpu.VMEM)],
        out_specs=pl.BlockSpec(memory_space=pltpu.VMEM),
        out_shape=jax.ShapeDtypeStruct((blocks, 2 * LANES), jnp.bfloat16),
        scratch_shapes=row_scratch(blocks, capacity, 2),
        compiler_params=pltpu.CompilerParams(vmem_limit_bytes=GRANT << 20),
        name=f"sum_rows_{capacity}",
    )(want, inbound)


def exchange(x):
    return lax.all_to_all(x, AXES, split_axis=0, concat_axis=0, tiled=True)


def per_device(tiles, tile_rows, tile_cols, tile_count, block_perm, panel):
    devices = lax.axis_size(AXES)
    held = panel.shape[0]
    blocks = devices * held
    slot_ids = jnp.arange(tiles.shape[0], dtype=jnp.int32)
    is_live = slot_ids < tile_count[0]
    stored_at = block_perm[tile_cols]
    wanted, slot_of, is_first = distinct_blocks(stored_at, is_live, blocks)

    digits = jnp.stack([wanted // held, wanted % held]).astype(jnp.bfloat16)
    stripes = panel.reshape(held, devices, 2, LANES).transpose(1, 2, 0, 3).reshape(devices, 2 * held, LANES)
    stripes = jnp.concatenate([stripes, jnp.broadcast_to(digits[None], (devices, 2, LANES))], axis=1)
    striped = exchange(stripes)
    lists = striped[:, 2 * held :, :].astype(jnp.int32)
    want = (lists[:, 0] * held + lists[:, 1])
    counts = jnp.sum((want < blocks).astype(jnp.int32), axis=1)
    want = (2 * want).reshape(devices // CHUNK, CHUNK, LANES)

    def with_capacity(capacity):
        def run():
            outgoing = gather_rows(want, striped, capacity)
            fetched = exchange(outgoing.reshape(devices, capacity, 2 * LANES))
            sketch, outbound = tile_products(
                slot_of, is_first, tile_rows, tile_count, tiles,
                fetched.reshape(devices * capacity, 2 * LANES), capacity,
            )
            inbound = exchange(outbound.reshape(devices, capacity, 2 * LANES))
            summed = sum_rows(want, inbound.reshape(devices * capacity, 2 * LANES), capacity, devices)
            return sketch, summed

        return run

    most = jnp.max(counts)
    choice = sum((most > c).astype(jnp.int32) for c in CAPACITIES[:-1])
    sketch, summed = lax.switch(choice, [with_capacity(c) for c in CAPACITIES])
    gram = exchange(summed.reshape(devices, held, 2 * LANES))
    return sketch, gram.transpose(1, 0, 2).astype(jnp.float32)


def solution(mesh):
    split = P(AXES, None, None)
    line = P(AXES)
    return jax.shard_map(
        per_device,
        mesh=mesh,
        in_specs=(split, line, line, line, P(), split),
        out_specs=(split, split),
        check_vma=False,
    )
```

time: 322 us -> 289 us (0.90)
  Pallas kernels: 67.5 us -> 35 us
    pallas_call x3, Pallas kernels: 67.5 us -> 35 us  [the longest x1 12.9 us: tile_products(): pl.pallas_call(functools.partial(product_kernel, capacity), in_specs=[pl....]
where the time goes in v1:
time: 289 us; the launch traced here: 288 us
  blocking collectives  238 us (82%)
  Pallas kernels  35 us (12%)
  local copies, waits for them, and re-layouts  6.32 us (2%)
  other arithmetic  4.8 us (2%)
    all_to_all x4, blocking collectives, exchange(): return lax.all_to_all(x, AXES, split_axis=0, concat_axis=0, tiled=True)  238 us
    pallas_call x1, Pallas kernels, tile_products(): pl.pallas_call(functools.partial(product_kernel, capacity), in_specs=[pl....  12.9 us
    pallas_call x1, Pallas kernels, sum_rows(): pl.pallas_call(functools.partial(sum_kernel, capacity), in_specs=[pl.Bloc...  12.4 us
    pallas_call x1, Pallas kernels, gather_rows(): pl.pallas_call(functools.partial(gather_kernel, capacity), in_specs=[pl.B...  9.81 us

profile of v1, /device:TPU:1, one launch (start us, length us, event | category | flops | bytes accessed | tf_op | source)
XLA Modules:
  0.0 288.0 jit_solution(15251718632260605697)
XLA Ops:
  0.6 0.0 copy-start
  1.3 0.7 compare_select_fusion.1
  2.0 0.0 copy-done
  2.0 1.1 gather_fusion
  3.1 0.2 select_reduce_fusion.1
  3.3 0.2 convert_reduce_fusion
  3.5 0.1 select_reduce_fusion
  3.7 1.3 reshape.178
  5.0 1.2 copy.11
  6.3 0.0 copy-start.5
  6.3 0.2 pad_maximum_fusion
  6.5 33.4 %all_to_all.40 = bf16[128,34,128]{2,1,0:T(8,128)(2,1)S(1)} all-to-all(bf16[128,34,128]{2,1,0:T(8,128)(2,1)S(1)} %pad_maximum_fusion), channel_id=1, replica_groups=mesh['rows'=32,'grp'=4] {'rows','grp'}, dimensions={0} | all-to-all | bytes 2228224 | tf_op jit(solution)/shard_map/all_to_all | solution.py:284
  39.9 0.1 slice_convert_fusion
  39.9 0.1 broadcast_multiply_fusion
  40.1 2.4 fusion
  42.4 0.6 reduce_max.22
  44.4 0.0 copy-done.5
  44.4 217.7 %conditional.1 = (bf16[48,128,256]{2,1,0:T(8,128)(2,1)}, bf16[2048,256]{1,0:T(8,128)(2,1)S(1)}) conditional(s32[]{:T(128)} %clamp.3, (s32[16,8,128]{2,1,0:T(8,128)S(1)}, bf16[128,34,128]{2,1,0:T(8,128)(2,1)S(1)}, s32[128]{0:T(128)S(1)}, s32[128]{0:T(128)S(1)}, s32[128]{0:T(128)S(1)}, /*index=5*/s32[1]{0:T(128)}, ...), branch_computations={%region_5.6_spmd, %region_6.7_spmd, %region_7.8_spmd} | conditional | bytes 50331692 | solution.py:321
  44.6 9.8 %gather_rows_112.1 = bf16[14336,256]{1,0:T(8,128)(2,1)S(1)} custom-call(s32[16,8,128]{2,1,0:T(8,128)S(1)} %get-tuple-element.56.want_ref, bf16[128,34,128]{2,1,0:T(8,128)(2,1)S(1)} %get-tuple-element.57.rows_ref), custom_call_target="tpu_custom_call" | custom-call | tf_op jit(solution)/shard_map/cond/branch_1_fun/gather_rows_112/pallas_call | solution.py:109
  54.4 0.0 copy-start.3
  54.4 90.4 %all_to_all.36 = bf16[128,112,256]{2,1,0:T(8,128)(2,1)S(1)} all-to-all(bf16[128,112,256]{2,1,0:T(8,128)(2,1)S(1)} %bitcast.37), channel_id=1, replica_groups=mesh['rows'=32,'grp'=4] {'rows','grp'}, dimensions={0} | all-to-all | bytes 14680064 | tf_op jit(solution)/shard_map/cond/branch_1_fun/all_to_all | solution.py:284
  144.8 0.0 copy-done.3
  144.8 12.9 %tile_products_112.1 = (bf16[48,128,256]{2,1,0:T(8,128)(2,1)}, bf16[14336,256]{1,0:T(8,128)(2,1)S(1)}) custom-call(s32[128]{0:T(128)S(1)} %get-tuple-element.51.slot_ref, s32[128]{0:T(128)S(1)} %get-tuple-element.52.first_ref, s32[128]{0:T(128)S(1)} %get-tuple-element.53.row_ref, s32[1]{0:T(128)} %get-tuple-element.54.count_ref, ...), custom_call_target="tpu_custom_call" | custom-call | tf_op jit(solution)/shard_map/cond/branch_1_fun/tile_products_112/pallas_call | solution.py:202
  157.6 91.5 %all_to_all.37 = bf16[128,112,256]{2,1,0:T(8,128)(2,1)S(1)} all-to-all(bf16[128,112,256]{2,1,0:T(8,128)(2,1)S(1)} %bitcast.42), channel_id=1, replica_groups=mesh['rows'=32,'grp'=4] {'rows','grp'}, dimensions={0} | all-to-all | bytes 14680064 | tf_op jit(solution)/shard_map/cond/branch_1_fun/all_to_all | solution.py:284
  249.2 12.4 %sum_rows_112.1 = bf16[2048,256]{1,0:T(8,128)(2,1)S(1)} custom-call(s32[16,8,128]{2,1,0:T(8,128)S(1)} %get-tuple-element.56.want_ref, bf16[14336,256]{1,0:T(8,128)(2,1)S(1)} %bitcast.36), custom_call_target="tpu_custom_call" | custom-call | tf_op jit(solution)/shard_map/cond/branch_1_fun/sum_rows_112/pallas_call | solution.py:272
  262.0 0.0 copy-start.1
  262.0 23.1 %all_to_all.41 = bf16[128,16,256]{2,1,0:T(8,128)(2,1)S(1)} all-to-all(bf16[128,16,256]{2,1,0:T(8,128)(2,1)S(1)} %bitcast.44), channel_id=1, replica_groups=mesh['rows'=32,'grp'=4] {'rows','grp'}, dimensions={0} | all-to-all | bytes 2097152 | tf_op jit(solution)/shard_map/all_to_all | solution.py:284
  285.2 0.3 convert_bitcast_fusion
  285.4 2.5 copy.12
  288.0 0.0 copy-done.1
  (7 shorter events, 0.1 us)
Async XLA Ops:
  0.6 1.4 copy-start
  6.3 38.1 %copy-start.5 = (s32[128]{0:T(128)S(1)}, s32[128]{0:T(128)}, u32[]{:S(2)}) copy-start(s32[128]{0:T(128)} %param.10) | copy-start | bytes 1540
  54.4 90.4 %copy-start.3 = (bf16[128,128,128]{2,1,0:T(8,128)(2,1)S(1)}, bf16[128,128,128]{2,1,0:T(8,128)(2,1)}, u32[]{:S(2)}) copy-start(bf16[128,128,128]{2,1,0:T(8,128)(2,1)} %get-tuple-element.55.tiles_ref) | copy-start | bytes 12582916 | tf_op jit(solution)/shard_map/cond
  262.0 26.0 %copy-start.1 = (s32[2048]{0:T(1024)S(1)}, s32[2048]{0:T(1024)}, u32[]{:S(2)}) copy-start(s32[2048]{0:T(1024)} %param.13) | copy-start | bytes 24580

commit v2 on v1

--- a/solution.py
+++ b/solution.py
@@ -14,8 +14,8 @@
 GROUP_BITS = 3
 SUM_GROUP = 8
 GRANT = 12
-PRODUCT_GRANT = 24
-CAPACITIES = (104, 112, 128)
+PRODUCT_GRANT = 28
+CAPACITIES = (104, 108, 112, 128)
 
 
 def distinct_blocks(stored_at, is_live, total_blocks):
@@ -33,10 +33,11 @@
 
 
 def chunk_lists(want_ref, buffers, semaphores, work):
-    chunks = want_ref.shape[0]
+    chunks = want_ref.shape[0] // CHUNK
 
     def copy(chunk, side):
-        return pltpu.make_async_copy(want_ref.at[chunk], buffers[side], semaphores.at[side])
+        source = want_ref.at[pl.ds(pl.multiple_of(chunk * CHUNK, CHUNK), CHUNK)]
+        return pltpu.make_async_copy(source, buffers[side], semaphores.at[side])
 
     for side in range(2):
         copy(side, side).start()
@@ -68,10 +69,14 @@
         pl.when(listed[local, start] < absent)(work)
 
 
-def gather_kernel(capacity, want_ref, rows_ref, out_ref, table, stage, list_a, list_b, semaphores):
+def gather_kernel(capacity, rows_ref, out_ref, want_ref, table, digits, stage, list_a, list_b, semaphores):
     devices, held = rows_ref.shape[0], 16
     blocks = devices * held
-    span = CHUNK * capacity
+    span = 2 * CHUNK * capacity
+    digits[...] = rows_ref[:, 2 * held :, :].astype(jnp.float32).reshape(devices * 8, LANES)
+    high = digits[pl.ds(0, devices, stride=8), :]
+    low = digits[pl.ds(1, devices, stride=8), :]
+    want_ref[...] = (2 * (high * held + low)).astype(jnp.int32)
     for half in range(2):
         rows = rows_ref[:, half * held : (half + 1) * held, :].astype(jnp.float32)
         table[pl.ds(half, blocks, stride=2), :] = rows.reshape(blocks, LANES)
@@ -86,66 +91,70 @@
                         stage[pl.ds(2 * (local * capacity + k), 2), :] = table[pl.ds(src, 2), :]
 
                 when_listed(listed, local, start, 2 * blocks, rows)
-        at = pl.multiple_of(chunk * span, 16)
-        out_ref[pl.ds(at, span), :LANES] = stage[pl.ds(0, span, stride=2), :].astype(jnp.bfloat16)
-        out_ref[pl.ds(at, span), LANES:] = stage[pl.ds(1, span, stride=2), :].astype(jnp.bfloat16)
+        out_ref[pl.ds(pl.multiple_of(chunk * span, 16), span), :] = stage[...].astype(jnp.bfloat16)
 
     chunk_lists(want_ref, (list_a, list_b), semaphores, work)
 
 
-def row_scratch(blocks, capacity, tables=1):
+def row_table(blocks):
+    return pltpu.VMEM((2 * (blocks + 8), LANES), jnp.float32)
+
+
+def list_scratch(capacity):
     lists = pltpu.SMEM((CHUNK, LANES), jnp.int32)
-    table = pltpu.VMEM((2 * (blocks + 8), LANES), jnp.float32)
-    return [table] * tables + [
-        pltpu.VMEM((2 * CHUNK * capacity, LANES), jnp.float32),
-        lists,
-        lists,
-        pltpu.SemaphoreType.DMA((2,)),
-    ]
-
-
-def gather_rows(want, rows, capacity):
+    stage = pltpu.VMEM((2 * CHUNK * capacity, LANES), jnp.float32)
+    return [stage, lists, lists, pltpu.SemaphoreType.DMA((2,))]
+
+
+def gather_rows(rows, capacity):
     devices = rows.shape[0]
     return pl.pallas_call(
         functools.partial(gather_kernel, capacity),
-        in_specs=[pl.BlockSpec(memory_space=pl.ANY), pl.BlockSpec(memory_space=pltpu.VMEM)],
-        out_specs=pl.BlockSpec(memory_space=pltpu.VMEM),
-        out_shape=jax.ShapeDtypeStruct((devices * capacity, 2 * LANES), jnp.bfloat16),
-        scratch_shapes=row_scratch(devices * 16, capacity),
+        in_specs=[pl.BlockSpec(memory_space=pltpu.VMEM)],
+        out_specs=[pl.BlockSpec(memory_space=pltpu.VMEM)] * 2,
+        out_shape=[
+            jax.ShapeDtypeStruct((devices * 2 * capacity, LANES), jnp.bfloat16),
+            jax.ShapeDtypeStruct((devices, LANES), jnp.int32),
+        ],
+        scratch_shapes=[row_table(devices * 16), pltpu.VMEM((devices * 8, LANES), jnp.float32)]
+        + list_scratch(capacity),
         compiler_params=pltpu.CompilerParams(vmem_limit_bytes=GRANT << 20),
         name=f"gather_rows_{capacity}",
-    )(want, rows)
+    )(rows)
 
 
 def product_kernel(
     capacity, slot_ref, first_ref, row_ref, count_ref, tiles_ref, in_ref, sketch_ref, out_ref,
-    in_l, in_r, acc, sketch, sent
+    spread_rows, acc, sketch, sent
 ):
-    stride = capacity + 1
+    width = 2 * capacity
+    stride = width + 1
     count = count_ref[0]
     full = lax.shift_right_logical(count, GROUP_BITS)
     group = 1 << GROUP_BITS
-    halves = ((in_l, pl.ds(0, LANES)), (in_r, pl.ds(LANES, LANES)))
 
     def spread(c, carry):
         for k in range(CHUNK):
-            source = pl.ds(pl.multiple_of((c * CHUNK + k) * capacity, 8), capacity)
-            for half, lanes in halves:
-                half[pl.ds((c * CHUNK + k) * stride, capacity), :] = in_ref[source, lanes].astype(jnp.float32)
+            j = c * CHUNK + k
+            source = pl.ds(pl.multiple_of(j * width, 8), width)
+            spread_rows[pl.ds(j * stride, width), :] = in_ref[source, :].astype(jnp.float32)
         return carry
 
     def pack(c, carry):
         for k in range(CHUNK):
-            target = pl.ds(pl.multiple_of((c * CHUNK + k) * capacity, 8), capacity)
-            for half, lanes in halves:
-                out_ref[target, lanes] = half[pl.ds((c * CHUNK + k) * stride, capacity), :].astype(jnp.bfloat16)
+            j = c * CHUNK + k
+            target = pl.ds(pl.multiple_of(j * width, 8), width)
+            out_ref[target, :] = spread_rows[pl.ds(j * stride, width), :].astype(jnp.bfloat16)
         return carry
+
+    def block_rows(t):
+        return [pl.ds(2 * slot_ref[t] + half, LANES, stride=stride) for half in range(2)]
 
     def forward(first_tile, group):
         products = []
         for t in [first_tile + k for k in range(group)]:
-            rows = pl.ds(slot_ref[t], LANES, stride=stride)
-            block = jnp.concatenate([half[rows, :].astype(jnp.bfloat16) for half, _ in halves], axis=1)
+            block = [spread_rows[rows, :].astype(jnp.bfloat16) for rows in block_rows(t)]
+            block = jnp.concatenate(block, axis=1)
             products.append(jnp.dot(tiles_ref[t], block, preferred_element_type=jnp.float32))
         total = acc[...]
         for k, product in enumerate(products):
@@ -169,10 +178,9 @@
             )
         for k, part in enumerate(parts):
             t = first_tile + k
-            rows = pl.ds(slot_ref[t], LANES, stride=stride)
             first = first_ref[t] == 1
-            for (half, _), piece in zip(halves, (part[:, :LANES], part[:, LANES:])):
-                half[rows, :] = piece + jnp.where(first, 0.0, half[rows, :])
+            for rows, piece in zip(block_rows(t), (part[:, :LANES], part[:, LANES:])):
+                spread_rows[rows, :] = piece + jnp.where(first, 0.0, spread_rows[rows, :])
 
     def over_tiles(work):
         def many(g, carry):
@@ -197,7 +205,6 @@
 
 
 def tile_products(slot_of, is_first, tile_rows, tile_count, tiles, fetched, capacity):
-    f32_rows = pltpu.VMEM((LANES * (capacity + 1), LANES), jnp.float32)
     sketch = (RB_DEV, LANES, 2 * LANES)
     return pl.pallas_call(
         functools.partial(product_kernel, capacity),
@@ -206,11 +213,10 @@
         out_specs=[pl.BlockSpec(memory_space=pl.ANY), pl.BlockSpec(memory_space=pltpu.VMEM)],
         out_shape=[
             jax.ShapeDtypeStruct(sketch, jnp.bfloat16),
-            jax.ShapeDtypeStruct((LANES * capacity, 2 * LANES), jnp.bfloat16),
+            jax.ShapeDtypeStruct(fetched.shape, jnp.bfloat16),
         ],
         scratch_shapes=[
-            f32_rows,
-            f32_rows,
+            pltpu.VMEM((LANES * (2 * capacity + 1) + 8, LANES), jnp.float32),
             pltpu.VMEM((LANES, 2 * LANES), jnp.float32),
             pltpu.VMEM(sketch, jnp.bfloat16),
             pltpu.SemaphoreType.DMA,
@@ -221,17 +227,15 @@
 
 
 def sum_kernel(capacity, want_ref, in_ref, out_ref, even, odd, stage, list_a, list_b, semaphores):
-    span = CHUNK * capacity
+    span = 2 * CHUNK * capacity
     blocks = out_ref.shape[0]
     even[...] = jnp.zeros_like(even)
     odd[...] = jnp.zeros_like(odd)
+    totals = (even, odd)
 
     def work(chunk, listed):
-        at = pl.multiple_of(chunk * span, 16)
-        stage[pl.ds(0, span, stride=2), :] = in_ref[pl.ds(at, span), :LANES].astype(jnp.float32)
-        stage[pl.ds(1, span, stride=2), :] = in_ref[pl.ds(at, span), LANES:].astype(jnp.float32)
+        stage[...] = in_ref[pl.ds(pl.multiple_of(chunk * span, 16), span), :].astype(jnp.float32)
         for local in range(0, CHUNK, 2):
-            totals = (even, odd)
 
             def load(side, g, stop, local=local):
                 loaded = []
@@ -267,14 +271,14 @@
         out_ref[:, half * LANES : (half + 1) * LANES] = (even[rows, :] + odd[rows, :]).astype(jnp.bfloat16)
 
 
-def sum_rows(want, inbound, capacity, devices):
-    blocks = devices * 16
+def sum_rows(want, inbound, capacity):
+    blocks = want.shape[0] * 16
     return pl.pallas_call(
         functools.partial(sum_kernel, capacity),
-        in_specs=[pl.BlockSpec(memory_space=pl.ANY), pl.BlockSpec(memory_space=pltpu.VMEM)],
+        in_specs=[pl.BlockSpec(memory_space=pltpu.VMEM)] * 2,
         out_specs=pl.BlockSpec(memory_space=pltpu.VMEM),
         out_shape=jax.ShapeDtypeStruct((blocks, 2 * LANES), jnp.bfloat16),
-        scratch_shapes=row_scratch(blocks, capacity, 2),
+        scratch_shapes=[row_table(blocks)] * 2 + list_scratch(capacity),
         compiler_params=pltpu.CompilerParams(vmem_limit_bytes=GRANT << 20),
         name=f"sum_rows_{capacity}",
     )(want, inbound)
@@ -293,30 +297,26 @@
     stored_at = block_perm[tile_cols]
     wanted, slot_of, is_first = distinct_blocks(stored_at, is_live, blocks)
 
-    digits = jnp.stack([wanted // held, wanted % held]).astype(jnp.bfloat16)
+    listed = jnp.sum(is_first)
+    notes = [wanted // held, wanted % held, jnp.full_like(wanted, listed)]
+    notes = jnp.stack(notes + [jnp.zeros_like(wanted)] * 5).astype(jnp.bfloat16)
     stripes = panel.reshape(held, devices, 2, LANES).transpose(1, 2, 0, 3).reshape(devices, 2 * held, LANES)
-    stripes = jnp.concatenate([stripes, jnp.broadcast_to(digits[None], (devices, 2, LANES))], axis=1)
+    stripes = jnp.concatenate([stripes, jnp.broadcast_to(notes[None], (devices, 8, LANES))], axis=1)
     striped = exchange(stripes)
-    lists = striped[:, 2 * held :, :].astype(jnp.int32)
-    want = (lists[:, 0] * held + lists[:, 1])
-    counts = jnp.sum((want < blocks).astype(jnp.int32), axis=1)
-    want = (2 * want).reshape(devices // CHUNK, CHUNK, LANES)
+    most = jnp.max(striped[:, 2 * held + 2, 0]).astype(jnp.int32)
 
     def with_capacity(capacity):
         def run():
-            outgoing = gather_rows(want, striped, capacity)
-            fetched = exchange(outgoing.reshape(devices, capacity, 2 * LANES))
+            outgoing, want = gather_rows(striped, capacity)
+            fetched = exchange(outgoing.reshape(devices, 2 * capacity, LANES))
             sketch, outbound = tile_products(
-                slot_of, is_first, tile_rows, tile_count, tiles,
-                fetched.reshape(devices * capacity, 2 * LANES), capacity,
+                slot_of, is_first, tile_rows, tile_count, tiles, fetched.reshape(outgoing.shape), capacity
             )
-            inbound = exchange(outbound.reshape(devices, capacity, 2 * LANES))
-            summed = sum_rows(want, inbound.reshape(devices * capacity, 2 * LANES), capacity, devices)
-            return sketch, summed
+            inbound = exchange(outbound.reshape(devices, 2 * capacity, LANES))
+            return sketch, sum_rows(want, inbound.reshape(outgoing.shape), capacity)
 
         return run
 
-    most = jnp.max(counts)
     choice = sum((most > c).astype(jnp.int32) for c in CAPACITIES[:-1])
     sketch, summed = lax.switch(choice, [with_capacity(c) for c in CAPACITIES])
     gram = exchange(summed.reshape(devices, held, 2 * LANES))

time: 289 us -> 274 us (0.948)
  blocking collectives: 238 us -> 228 us
    all_to_all x4, blocking collectives: 238 us -> 228 us  [exchange(): return lax.all_to_all(x, AXES, split_axis=0, concat_axis=0, tiled=True)]
where the time goes in v2:
time: 274 us
  blocking collectives  228 us (83%)
  Pallas kernels  33.5 us (12%)
  local copies, waits for them, and re-layouts  6.37 us (2%)
  other arithmetic  2.99 us (1%)
  between operations  2.75 us (1%)
    all_to_all x4, blocking collectives, exchange(): return lax.all_to_all(x, AXES, split_axis=0, concat_axis=0, tiled=True)  228 us
    pallas_call x1, Pallas kernels, tile_products(): pl.pallas_call(functools.partial(product_kernel, capacity), in_specs=[pl....  12.6 us
    pallas_call x1, Pallas kernels, sum_rows(): pl.pallas_call(functools.partial(sum_kernel, capacity), in_specs=[pl.Bloc...  11.7 us
    pallas_call x1, Pallas kernels, gather_rows(): pl.pallas_call(functools.partial(gather_kernel, capacity), in_specs=[pl.B...  9.11 us

profile of v2, /device:TPU:1, one launch (start us, length us, event | category | flops | bytes accessed | tf_op | source)
XLA Modules:
  0.0 274.5 jit_solution(18314946791808211460)
XLA Ops:
  0.6 0.0 copy-start
  1.3 0.7 compare_select_fusion.1
  2.0 0.0 copy-done
  2.0 1.1 gather_fusion
  3.1 0.2 select_reduce_fusion.1
  3.3 0.6 convert_reduce_fusion.1
  4.6 0.2 convert_reduce_fusion
  4.8 0.1 select_reduce_fusion
  5.0 1.3 reshape.188
  6.3 0.0 copy-start.6
  6.3 1.2 copy.11
  7.7 0.2 pad_maximum_fusion
  7.8 33.4 %all_to_all.50 = bf16[128,40,128]{2,1,0:T(8,128)(2,1)S(1)} all-to-all(bf16[128,40,128]{2,1,0:T(8,128)(2,1)S(1)} %pad_maximum_fusion), channel_id=1, replica_groups=mesh['rows'=32,'grp'=4] {'rows','grp'}, dimensions={0} | all-to-all | bytes 2621440 | tf_op jit(solution)/shard_map/all_to_all | solution.py:288
  41.2 0.7 slice_reduce_fusion
  42.6 0.0 copy-done.6
  42.6 206.1 %conditional.1 = (bf16[48,128,256]{2,1,0:T(8,128)(2,1)}, bf16[2048,256]{1,0:T(8,128)(2,1)S(1)}) conditional(s32[]{:T(128)} %clamp.3, (bf16[128,40,128]{2,1,0:T(8,128)(2,1)S(1)}, s32[128]{0:T(128)S(1)}, s32[128]{0:T(128)S(1)}, s32[128]{0:T(128)S(1)}, s32[1]{0:T(128)}, ...), branch_computations={%region_5.6_spmd, %region_6.7_spmd, %region_7.8_spmd, %region_8.9_... | conditional | bytes 50331692 | solution.py:321
  42.6 9.1 %gather_rows_104.1 = (bf16[26624,128]{1,0:T(8,128)(2,1)S(1)}, s32[128,128]{1,0:T(8,128)S(1)}) custom-call(bf16[128,40,128]{2,1,0:T(8,128)(2,1)S(1)} %get-tuple-element.53.rows_ref), custom_call_target="tpu_custom_call" | custom-call | tf_op jit(solution)/shard_map/cond/branch_0_fun/gather_rows_104/pallas_call | solution.py:111
  51.7 0.0 copy-start.2
  51.8 84.8 %all_to_all.42 = bf16[128,208,128]{2,1,0:T(8,128)(2,1)S(1)} all-to-all(bf16[128,208,128]{2,1,0:T(8,128)(2,1)S(1)} %bitcast.50), channel_id=1, replica_groups=mesh['rows'=32,'grp'=4] {'rows','grp'}, dimensions={0} | all-to-all | bytes 13631488 | tf_op jit(solution)/shard_map/cond/branch_0_fun/all_to_all | solution.py:288
  136.5 0.0 copy-done.2
  136.5 12.6 %tile_products_104.1 = (bf16[48,128,256]{2,1,0:T(8,128)(2,1)}, bf16[26624,128]{1,0:T(8,128)(2,1)S(1)}) custom-call(s32[128]{0:T(128)S(1)} %get-tuple-element.48.slot_ref, s32[128]{0:T(128)S(1)} %get-tuple-element.49.first_ref, s32[128]{0:T(128)S(1)} %get-tuple-element.50.row_ref, s32[1]{0:T(128)} %get-tuple-element.51.count_ref, ...), custom_call_target="tpu_custom_call" | custom-call | tf_op jit(solution)/shard_map/cond/branch_0_fun/tile_products_104/pallas_call | solution.py:209
  149.2 87.2 %all_to_all.43 = bf16[128,208,128]{2,1,0:T(8,128)(2,1)S(1)} all-to-all(bf16[128,208,128]{2,1,0:T(8,128)(2,1)S(1)} %bitcast.49), channel_id=1, replica_groups=mesh['rows'=32,'grp'=4] {'rows','grp'}, dimensions={0} | all-to-all | bytes 13631488 | tf_op jit(solution)/shard_map/cond/branch_0_fun/all_to_all | solution.py:288
  236.4 11.7 %sum_rows_104.1 = bf16[2048,256]{1,0:T(8,128)(2,1)S(1)} custom-call(s32[128,128]{1,0:T(8,128)S(1)} %get-tuple-element.56.want_ref, bf16[26624,128]{1,0:T(8,128)(2,1)S(1)} %bitcast.42), custom_call_target="tpu_custom_call" | custom-call | tf_op jit(solution)/shard_map/cond/branch_0_fun/sum_rows_104/pallas_call | solution.py:276
  248.7 0.0 copy-start.1
  248.7 22.9 %all_to_all.51 = bf16[128,16,256]{2,1,0:T(8,128)(2,1)S(1)} all-to-all(bf16[128,16,256]{2,1,0:T(8,128)(2,1)S(1)} %bitcast.51), channel_id=1, replica_groups=mesh['rows'=32,'grp'=4] {'rows','grp'}, dimensions={0} | all-to-all | bytes 2097152 | tf_op jit(solution)/shard_map/all_to_all | solution.py:288
  271.7 0.3 convert_bitcast_fusion
  271.9 2.5 copy.12
  274.5 0.0 copy-done.1
  (10 shorter events, 0.1 us)
Async XLA Ops:
  0.6 1.4 copy-start
  6.3 36.3 %copy-start.6 = (s32[128]{0:T(128)S(1)}, s32[128]{0:T(128)}, u32[]{:S(2)}) copy-start(s32[128]{0:T(128)} %param.11) | copy-start | bytes 1540
  51.7 84.8 %copy-start.2 = (bf16[128,128,128]{2,1,0:T(8,128)(2,1)S(1)}, bf16[128,128,128]{2,1,0:T(8,128)(2,1)}, u32[]{:S(2)}) copy-start(bf16[128,128,128]{2,1,0:T(8,128)(2,1)} %get-tuple-element.52.tiles_ref) | copy-start | bytes 12582916 | tf_op jit(solution)/shard_map/cond
  248.7 25.8 %copy-start.1 = (s32[2048]{0:T(1024)S(1)}, s32[2048]{0:T(1024)}, u32[]{:S(2)}) copy-start(s32[2048]{0:T(1024)} %param.14) | copy-start | bytes 24580

commit v3 on v2

--- a/solution.py
+++ b/solution.py
@@ -284,6 +284,81 @@
     )(want, inbound)
 
 
+def stripe_kernel(panel_ref, notes_ref, out_ref, rows):
+    held, devices = panel_ref.shape[0], panel_ref.shape[1]
+    stride = 2 * held + 1
+    for s in range(held):
+        for half in range(2):
+            piece = panel_ref[s, :, half * LANES : (half + 1) * LANES].astype(jnp.float32)
+            rows[pl.ds(half * held + s, devices, stride=stride), :] = piece
+
+    def write(c, carry):
+        for k in range(CHUNK):
+            i = c * CHUNK + k
+            out_ref[i, : 2 * held, :] = rows[pl.ds(i * stride, 2 * held), :].astype(jnp.bfloat16)
+            out_ref[i, 2 * held :, :] = notes_ref[...]
+        return carry
+
+    lax.fori_loop(0, devices // CHUNK, write, 0)
+
+
+def stripe_rows(panel, notes):
+    held, devices = panel.shape[0], panel.shape[1]
+    return pl.pallas_call(
+        stripe_kernel,
+        in_specs=[pl.BlockSpec(memory_space=pltpu.VMEM)] * 2,
+        out_specs=pl.BlockSpec(memory_space=pltpu.VMEM),
+        out_shape=jax.ShapeDtypeStruct((devices, 2 * held + 8, LANES), jnp.bfloat16),
+        scratch_shapes=[pltpu.VMEM((devices * (2 * held + 1) + 8, LANES), jnp.float32)],
+        compiler_params=pltpu.CompilerParams(vmem_limit_bytes=GRANT << 20),
+        name="stripe_rows",
+    )(panel, notes)
+
+
+def finish_kernel(in_ref, gram_ref, left, right, blocks, sent):
+    devices, held = in_ref.shape[0], in_ref.shape[1]
+    stride = held + 1
+    halves = (left, right)
+
+    def spread(c, carry):
+        for k in range(CHUNK):
+            i = c * CHUNK + k
+            for half in range(2):
+                piece = in_ref[i, :, half * LANES : (half + 1) * LANES].astype(jnp.float32)
+                halves[half][pl.ds(i * stride, held), :] = piece
+        return carry
+
+    lax.fori_loop(0, devices // CHUNK, spread, 0)
+    sends = []
+    for s in range(held):
+        for half in range(2):
+            piece = halves[half][pl.ds(s, devices, stride=stride), :]
+            blocks[s, :, half * LANES : (half + 1) * LANES] = piece
+        sends.append(pltpu.make_async_copy(blocks.at[s], gram_ref.at[s], sent.at[s]))
+        sends[-1].start()
+    for send in sends:
+        send.wait()
+
+
+def finish_gram(rows):
+    devices, held, width = rows.shape
+    half = pltpu.VMEM((devices * (held + 1) + 8, LANES), jnp.float32)
+    return pl.pallas_call(
+        finish_kernel,
+        in_specs=[pl.BlockSpec(memory_space=pltpu.VMEM)],
+        out_specs=pl.BlockSpec(memory_space=pl.ANY),
+        out_shape=jax.ShapeDtypeStruct((held, devices, width), jnp.float32),
+        scratch_shapes=[
+            half,
+            half,
+            pltpu.VMEM((held, devices, width), jnp.float32),
+            pltpu.SemaphoreType.DMA((held,)),
+        ],
+        compiler_params=pltpu.CompilerParams(vmem_limit_bytes=GRANT << 20),
+        name="finish_gram",
+    )(rows)
+
+
 def exchange(x):
     return lax.all_to_all(x, AXES, split_axis=0, concat_axis=0, tiled=True)
 
@@ -297,13 +372,11 @@
     stored_at = block_perm[tile_cols]
     wanted, slot_of, is_first = distinct_blocks(stored_at, is_live, blocks)
 
-    listed = jnp.sum(is_first)
-    notes = [wanted // held, wanted % held, jnp.full_like(wanted, listed)]
-    notes = jnp.stack(notes + [jnp.zeros_like(wanted)] * 5).astype(jnp.bfloat16)
-    stripes = panel.reshape(held, devices, 2, LANES).transpose(1, 2, 0, 3).reshape(devices, 2 * held, LANES)
-    stripes = jnp.concatenate([stripes, jnp.broadcast_to(notes[None], (devices, 8, LANES))], axis=1)
-    striped = exchange(stripes)
-    most = jnp.max(striped[:, 2 * held + 2, 0]).astype(jnp.int32)
+    notes = jnp.stack([wanted // held, wanted % held] + [jnp.zeros_like(wanted)] * 6)
+    striped = exchange(stripe_rows(panel, notes.astype(jnp.bfloat16)))
+    nearest = jnp.min(striped[:, 2 * held, :].astype(jnp.float32), axis=0)
+    marks = functools.reduce(jnp.logical_or, [slot_ids == c for c in CAPACITIES[:-1]])
+    choice = jnp.sum((marks & (nearest < devices)).astype(jnp.int32))
 
     def with_capacity(capacity):
         def run():
@@ -317,10 +390,9 @@
 
         return run
 
-    choice = sum((most > c).astype(jnp.int32) for c in CAPACITIES[:-1])
     sketch, summed = lax.switch(choice, [with_capacity(c) for c in CAPACITIES])
     gram = exchange(summed.reshape(devices, held, 2 * LANES))
-    return sketch, gram.transpose(1, 0, 2).astype(jnp.float32)
+    return sketch, finish_gram(gram)
 
 
 def solution(mesh):

time: 274 us -> 274 us (level); the launches traced: 274 us -> 271 us
  local copies, waits for them, and re-layouts: 6.37 us -> 2.57 us
where the time goes in v3:
time: 274 us; the launch traced here: 271 us
  blocking collectives  228 us (83%)
  Pallas kernels  35.8 us (13%)
    all_to_all x4, blocking collectives, exchange(): return lax.all_to_all(x, AXES, split_axis=0, concat_axis=0, tiled=True)  228 us
    pallas_call x1, Pallas kernels, tile_products(): pl.pallas_call(functools.partial(product_kernel, capacity), in_specs=[pl....  12.9 us
    pallas_call x1, Pallas kernels, sum_rows(): pl.pallas_call(functools.partial(sum_kernel, capacity), in_specs=[pl.Bloc...  11.8 us
    pallas_call x1, Pallas kernels, gather_rows(): pl.pallas_call(functools.partial(gather_kernel, capacity), in_specs=[pl.B...  9.17 us

profile of v3, /device:TPU:1, one launch (start us, length us, event | category | flops | bytes accessed | tf_op | source)
XLA Modules:
  0.0 270.9 jit_solution(10460245685936582547)
XLA Ops:
  0.6 0.0 copy-start
  1.3 0.7 compare_select_fusion.1
  2.0 0.1 pad.3.clone
  2.1 0.1 pad.2.clone
  2.1 0.0 copy-done
  2.1 1.1 gather_fusion
  3.3 0.2 select_reduce_fusion.1
  3.5 0.2 convert_reduce_fusion
  3.7 0.1 select_reduce_fusion
  3.8 0.1 maximum_maximum_fusion.notes_ref
  3.9 0.0 copy-start.2
  3.9 1.2 copy-done.2
  5.1 0.3 stripe_rows.1
  5.5 33.4 %all_to_all.50 = bf16[128,40,128]{2,1,0:T(8,128)(2,1)S(1)} all-to-all(bf16[128,40,128]{2,1,0:T(8,128)(2,1)S(1)} %stripe_rows.1), channel_id=1, replica_groups=mesh['rows'=32,'grp'=4] {'rows','grp'}, dimensions={0} | all-to-all | bytes 2621440 | tf_op jit(solution)/shard_map/all_to_all | solution.py:363
  38.8 0.2 fusion
  39.0 0.6 fusion.4
  40.3 205.8 %conditional.1 = (bf16[48,128,256]{2,1,0:T(8,128)(2,1)}, bf16[2048,256]{1,0:T(8,128)(2,1)S(1)}) conditional(s32[]{:T(128)} %clamp.3, (bf16[128,40,128]{2,1,0:T(8,128)(2,1)S(1)}, s32[128]{0:T(128)S(1)}, s32[128]{0:T(128)S(1)}, s32[128]{0:T(128)}, s32[1]{0:T(128)}, ...), branch_computations={%region_5.6_spmd, %region_6.7_spmd, %region_7.8_spmd, %region_8.9_... | conditional | bytes 50333768 | solution.py:393
  40.3 9.2 %gather_rows_104.1 = (bf16[26624,128]{1,0:T(8,128)(2,1)S(1)}, s32[128,128]{1,0:T(8,128)S(1)}) custom-call(bf16[128,40,128]{2,1,0:T(8,128)(2,1)S(1)} %get-tuple-element.53.rows_ref), custom_call_target="tpu_custom_call" | custom-call | tf_op jit(solution)/shard_map/cond/branch_0_fun/gather_rows_104/pallas_call | solution.py:111
  49.5 0.0 copy-start.3
  49.5 0.0 copy-start.7
  49.5 84.8 %all_to_all.42 = bf16[128,208,128]{2,1,0:T(8,128)(2,1)S(1)} all-to-all(bf16[128,208,128]{2,1,0:T(8,128)(2,1)S(1)} %bitcast.45), channel_id=1, replica_groups=mesh['rows'=32,'grp'=4] {'rows','grp'}, dimensions={0} | all-to-all | bytes 13631488 | tf_op jit(solution)/shard_map/cond/branch_0_fun/all_to_all | solution.py:363
  134.3 0.0 copy-done.3
  134.3 0.0 copy-done.7
  134.3 12.9 %tile_products_104.1 = (bf16[48,128,256]{2,1,0:T(8,128)(2,1)}, bf16[26624,128]{1,0:T(8,128)(2,1)S(1)}) custom-call(s32[128]{0:T(128)S(1)} %get-tuple-element.48.slot_ref, s32[128]{0:T(128)S(1)} %get-tuple-element.49.first_ref, s32[128]{0:T(128)S(1)} %copy-done.7, s32[1]{0:T(128)} %get-tuple-element.51.count_ref, bf16[128,128,128]{2,1,0:T(8,128)(2,1)S(1)} %copy-done.3, ...), custom_call_target="tpu_custom_call" | custom-call | tf_op jit(solution)/shard_map/cond/branch_0_fun/tile_products_104/pallas_call | solution.py:209
  147.2 86.7 %all_to_all.43 = bf16[128,208,128]{2,1,0:T(8,128)(2,1)S(1)} all-to-all(bf16[128,208,128]{2,1,0:T(8,128)(2,1)S(1)} %bitcast.44), channel_id=1, replica_groups=mesh['rows'=32,'grp'=4] {'rows','grp'}, dimensions={0} | all-to-all | bytes 13631488 | tf_op jit(solution)/shard_map/cond/branch_0_fun/all_to_all | solution.py:363
  233.9 11.8 %sum_rows_104.1 = bf16[2048,256]{1,0:T(8,128)(2,1)S(1)} custom-call(s32[128,128]{1,0:T(8,128)S(1)} %get-tuple-element.56.want_ref, bf16[26624,128]{1,0:T(8,128)(2,1)S(1)} %bitcast.37), custom_call_target="tpu_custom_call" | custom-call | tf_op jit(solution)/shard_map/cond/branch_0_fun/sum_rows_104/pallas_call | solution.py:276
  246.1 0.0 copy-start.1
  246.1 22.9 %all_to_all.51.in_ref = bf16[128,16,256]{2,1,0:T(8,128)(2,1)S(1)} all-to-all(bf16[128,16,256]{2,1,0:T(8,128)(2,1)S(1)} %bitcast.46), channel_id=1, replica_groups=mesh['rows'=32,'grp'=4] {'rows','grp'}, dimensions={0} | all-to-all | bytes 2097152 | tf_op jit(solution)/shard_map/all_to_all | solution.py:363
  269.1 1.6 finish_gram.1
  270.7 0.0 copy-done.1
  (7 shorter events, 0.0 us)
Async XLA Ops:
  0.6 1.5 copy-start
  3.9 1.2 copy-start.2
  49.5 84.8 %copy-start.3 = (bf16[128,128,128]{2,1,0:T(8,128)(2,1)S(1)}, bf16[128,128,128]{2,1,0:T(8,128)(2,1)}, u32[]{:S(2)}) copy-start(bf16[128,128,128]{2,1,0:T(8,128)(2,1)} %get-tuple-element.52.tiles_ref) | copy-start | bytes 12582916 | tf_op jit(solution)/shard_map/cond
  49.5 84.8 %copy-start.7 = (s32[128]{0:T(128)S(1)}, s32[128]{0:T(128)}, u32[]{:S(2)}) copy-start(s32[128]{0:T(128)} %get-tuple-element.50.row_ref) | copy-start | bytes 1540 | tf_op jit(solution)/shard_map/cond
  246.1 24.6 %copy-start.1 = (s32[2048]{0:T(1024)S(1)}, s32[2048]{0:T(1024)}, u32[]{:S(2)}) copy-start(s32[2048]{0:T(1024)} %param.14) | copy-start | bytes 24580
